TPU v7x, 128 devices: a whole 4x4x4 slice. The times are simulated.
128 devices in a mesh: seq: 16 (over x, y), tp: 8 (over z, core).
Axes of the slice: x: 4, y: 4, z: 4, core: 2. Of those that a mesh axis runs over, the one named last changes fastest.
Arguments:
- patches: bfloat16 [8192, 1280], P('seq'), may hold values from -6 to 6
- image_ids: int32 [2048], replicated, may hold values from 0 to 31, never falling along the last dimension, each value on 1 to 128 neighbouring positions
- vision_gain: float32 [1280], replicated, may hold values from 0.5 to 2
- v_query: bfloat16 [1280, 1280], P(None, 'tp'), may hold values from -0.15625 to 0.15625
- v_key: bfloat16 [1280, 1280], P(None, 'tp'), may hold values from -0.15625 to 0.15625
- v_value: bfloat16 [1280, 1280], P(None, 'tp'), may hold values from -0.15625 to 0.15625
- v_out: bfloat16 [1280, 1280], P('tp'), may hold values from -0.625 to 0.625
- merge_gain: float32 [1280], replicated, may hold values from 0.5 to 1.5
- merge_up: bfloat16 [5120, 5120], P('seq', 'tp'), may hold values from -0.078125 to 0.078125
- merge_down: bfloat16 [5120, 8192], P('tp', 'seq'), may hold values from -0.078125 to 0.078125
- owners: int32 [2048, 1], replicated, may hold values from 0 to 15; in each aligned block of 128 rows (0 to 127, 128 to 255, ...) at most 16 rows name the same one
- text_embed: bfloat16 [4096, 8192], P('seq', 'tp'), may hold values from -6 to 6
- segment_ids: int32 [4096], P('seq'), may hold values from 0 to 63, never falling along the last dimension, each value on 1 to 256 neighbouring positions
- lang_gain: float32 [8192], replicated, may hold values from 0.5 to 2
- l_query: bfloat16 [8192, 4096], P(None, 'tp'), may hold values from -0.0625 to 0.0625
- l_key: bfloat16 [8192, 1024], P(None, 'tp'), may hold values from -0.0625 to 0.0625
- l_value: bfloat16 [8192, 1024], P(None, 'tp'), may hold values from -0.0625 to 0.0625
- l_out: bfloat16 [4096, 8192], P('tp'), may hold values from -0.09375 to 0.09375
Outputs:
- layer_out: bfloat16 [4096, 8192], P('seq', 'tp')
Inputs may be any that keep to these rules, and one draw needn't show every extreme that they name: `image_ids`: never falling; each image spans 1 to 128 merged tokens, one exactly 128. `owners`: among the rows of one device (aligned blocks of 128 rows) at most 16 name the same packed sequence. `segment_ids`: never falling; each document holds 1 to 256 slots, one exactly 256.
All inputs are finite; a program needn't handle non-finite values.
Results may differ from a plain program's by a relative error of at most 0.019.
Values may be sent and summed in bfloat16 or wider, within the bound.
No kernel may reach another device: no remote copies, remote signals or barrier semaphores. Data moves between devices by JAX's collectives and lax.ppermute only.
A program may use at most 128 MiB of HBM per device.

v0:
```python
import math
import jax
import jax.numpy as jnp
from jax import lax
from jax.sharding import PartitionSpec as P

DV = 1280
VHEADS = 16
LHD = 128
EPSILON = 1e-06
NEG_FILL = -1e30


def extended(cells, sides, width):
    for axis, dim in sides:
        count = lax.axis_size(axis)
        ends = count - 1
        head = lax.slice_in_dim(cells, 0, width, axis=dim)
        tail = lax.slice_in_dim(cells, cells.shape[dim] - width, cells.shape[dim], axis=dim)
        cells = jnp.concatenate(
            [
                lax.ppermute(tail, axis, [(i, (i + 1) % count) for i in range(ends)]),
                cells,
                lax.ppermute(head, axis, [((i + 1) % count, i) for i in range(ends)]),
            ],
            axis=dim,
        )
    return cells


def split_up(value, dim, length):
    shape = value.shape
    pieces = value.reshape(*shape[:dim], length, shape[dim] // length, *shape[dim + 1 :])
    return jnp.moveaxis(pieces, dim, 0)


def sum_at_owner(value, axis, dim):
    pieces = split_up(value, dim, lax.axis_size(axis))
    arrived = lax.all_to_all(pieces, axis, split_axis=0, concat_axis=0, tiled=True)
    return arrived.astype(jnp.float32).sum(axis=0)


def from_everyone(value, axis):
    copies = jnp.broadcast_to(value, (lax.axis_size(axis), *value.shape))
    return lax.all_to_all(copies, axis, split_axis=0, concat_axis=0, tiled=True)


def of_everyone(value, axis):
    everything = from_everyone(value, axis)
    return jnp.sum(everything, axis=0)


def in_order(pieces, dim):
    pieces = jnp.moveaxis(pieces, 0, dim)
    shape = pieces.shape
    return pieces.reshape(*shape[:dim], shape[dim] * shape[dim + 1], *shape[dim + 2 :])


def gather_directly(value, axis, dim):
    pieces = from_everyone(value, axis)
    return in_order(pieces, dim)


def rms_scaled(values, norm_gain):
    mean_square = jnp.mean(values * values, axis=-1, keepdims=True)
    return (values * lax.rsqrt(mean_square + EPSILON) * norm_gain).astype(jnp.bfloat16)


def masked_attend(query_rows, key_rows, value_rows, allowed, score_scale):
    scores = (
        jnp.einsum("qhd,nhd->hqn", query_rows, key_rows, preferred_element_type=jnp.float32)
        * score_scale
    )
    scores = jnp.where(allowed[None], scores, NEG_FILL)
    highest = jnp.max(scores, axis=-1, keepdims=True)
    weights_raw = jnp.where(allowed[None], jnp.exp(scores - highest), 0.0)
    totals = jnp.sum(weights_raw, axis=-1)
    mixed = jnp.einsum(
        "hqn,nhd->qhd",
        weights_raw.astype(jnp.bfloat16),
        value_rows,
        preferred_element_type=jnp.float32,
    )
    mixed = mixed / jnp.transpose(totals)[:, :, None]
    return mixed.reshape(mixed.shape[0], -1).astype(jnp.bfloat16)


def body(
    patches,
    image_ids,
    vision_gain,
    v_query,
    v_key,
    v_value,
    v_out,
    merge_gain,
    merge_up,
    merge_down,
    owners,
    text_embed,
    segment_ids,
    lang_gain,
    l_query,
    l_key,
    l_value,
    l_out,
):
    row_count = patches.shape[0]
    local_width = v_query.shape[1]
    head_size = DV // VHEADS
    head_count = local_width // head_size
    score_scale = 1.0 / math.sqrt(head_size)
    seq_index = lax.axis_index("seq")
    patch_ids = jnp.repeat(image_ids, 4)
    my_ids = lax.dynamic_slice_in_dim(patch_ids, seq_index * row_count, row_count)
    vision_state = patches.astype(jnp.float32)
    normed = rms_scaled(vision_state, vision_gain)
    query_rows = jnp.dot(normed, v_query, preferred_element_type=jnp.float32).astype(jnp.bfloat16)
    key_part = jnp.dot(normed, v_key, preferred_element_type=jnp.float32).astype(jnp.bfloat16)
    value_part = jnp.dot(normed, v_value, preferred_element_type=jnp.float32).astype(jnp.bfloat16)
    key_value = jnp.concatenate([key_part, value_part], axis=1)
    query_grid = query_rows.reshape(row_count, head_count, head_size)
    nearby = extended(key_value, (("seq", 0),), row_count)
    padded_ids = jnp.pad(patch_ids, (row_count, row_count), constant_values=-1)
    nearby_ids = lax.dynamic_slice_in_dim(padded_ids, seq_index * row_count, 3 * row_count)
    allowed = my_ids[:, None] == nearby_ids[None, :]
    nearby_keys = nearby[:, :local_width].reshape(3 * row_count, head_count, head_size)
    nearby_values = nearby[:, local_width:].reshape(3 * row_count, head_count, head_size)
    attended = masked_attend(query_grid, nearby_keys, nearby_values, allowed, score_scale)
    partial_value = jnp.dot(attended, v_out, preferred_element_type=jnp.float32)
    share = sum_at_owner(partial_value.astype(jnp.bfloat16), "tp", 1)
    share_width = share.shape[1]
    tp_index = lax.axis_index("tp")
    own_state = (
        lax.dynamic_slice_in_dim(vision_state, tp_index * share_width, share_width, 1) + share
    )
    squares = of_everyone(jnp.sum(own_state * own_state, axis=1), "tp")
    gain_share = lax.dynamic_slice_in_dim(merge_gain, tp_index * share_width, share_width)
    normed_share = (own_state * lax.rsqrt(squares / DV + EPSILON)[:, None] * gain_share).astype(
        jnp.bfloat16
    )
    merge_normed = gather_directly(normed_share, "tp", 1)
    token_count = row_count // 4
    merge_rows = merge_normed.reshape(token_count, 4 * DV)
    hidden_sum = jnp.dot(
        merge_rows,
        lax.all_gather(merge_up, "seq", axis=0, tiled=True),
        preferred_element_type=jnp.float32,
    )
    hidden = jax.nn.gelu(hidden_sum, approximate=False).astype(jnp.bfloat16)
    down_terms = jnp.dot(
        hidden,
        lax.all_gather(merge_down, "seq", axis=1, tiled=True),
        preferred_element_type=jnp.float32,
    )
    merged = sum_at_owner(down_terms.astype(jnp.bfloat16), "tp", 1).astype(jnp.bfloat16)
    owner_count = lax.axis_size("seq")
    pair_cap = 2 * token_count // owner_count
    feature_width = merged.shape[1]
    owner_iota = jnp.arange(owner_count, dtype=jnp.int32)
    destination = owners[:, 0]
    one_hot = (destination[:, None] == owner_iota[None, :]).astype(jnp.int32)
    grid_counts = one_hot.reshape(owner_count, token_count, owner_count)
    pair_counts = jnp.sum(grid_counts, axis=1)
    mine = lax.dynamic_slice_in_dim(grid_counts, seq_index, 1, 0)[0]
    local_rank = jnp.sum((jnp.cumsum(mine, axis=0) - mine) * mine, axis=1)
    my_destination = lax.dynamic_slice_in_dim(destination, seq_index * token_count, token_count)
    send_index = my_destination * pair_cap + local_rank
    outgoing = (
        jnp.zeros((owner_count * pair_cap, feature_width), jnp.bfloat16).at[send_index].set(merged)
    )
    incoming = lax.all_to_all(
        outgoing.reshape(owner_count, pair_cap, feature_width),
        "seq",
        split_axis=0,
        concat_axis=0,
        tiled=True,
    )
    slot_count = text_embed.shape[0]
    from_each = lax.dynamic_slice_in_dim(pair_counts, seq_index, 1, 1)[:, 0]
    offsets = jnp.cumsum(from_each) - from_each
    pair_rank = jnp.arange(pair_cap, dtype=jnp.int32)
    placement = jnp.where(
        pair_rank[None, :] < from_each[:, None], offsets[:, None] + pair_rank[None, :], slot_count
    ).reshape(-1)
    vision_slots = (
        jnp.zeros((slot_count + 1, feature_width), jnp.bfloat16)
        .at[placement]
        .set(incoming.reshape(-1, feature_width))[:slot_count]
    )
    is_vision = jnp.arange(slot_count, dtype=jnp.int32) < jnp.sum(from_each)
    filled = jnp.where(is_vision[:, None], vision_slots, text_embed)
    full_rows = lax.all_gather(filled, "tp", axis=1, tiled=True)
    lang_normed = rms_scaled(full_rows.astype(jnp.float32), lang_gain)
    lang_query = jnp.dot(lang_normed, l_query, preferred_element_type=jnp.float32).astype(
        jnp.bfloat16
    )
    lang_key = jnp.dot(lang_normed, l_key, preferred_element_type=jnp.float32).astype(jnp.bfloat16)
    lang_value = jnp.dot(lang_normed, l_value, preferred_element_type=jnp.float32).astype(
        jnp.bfloat16
    )
    kv_heads = l_key.shape[1] // LHD
    group_size = l_query.shape[1] // LHD // kv_heads
    query_five = lang_query.reshape(slot_count, kv_heads, group_size, LHD)
    key_three = lang_key.reshape(slot_count, kv_heads, LHD)
    value_three = lang_value.reshape(slot_count, kv_heads, LHD)
    position = jnp.arange(slot_count, dtype=jnp.int32)
    allowed_lang = (segment_ids[:, None] == segment_ids[None, :]) & (
        position[None, :] <= position[:, None]
    )
    scores = jnp.einsum(
        "qkgd,nkd->kgqn", query_five, key_three, preferred_element_type=jnp.float32
    ) / math.sqrt(LHD)
    scores = jnp.where(allowed_lang[None, None], scores, NEG_FILL)
    highest = jnp.max(scores, axis=-1, keepdims=True)
    weights_raw = jnp.where(allowed_lang[None, None], jnp.exp(scores - highest), 0.0)
    totals = jnp.sum(weights_raw, axis=-1)
    mixed = jnp.einsum(
        "kgqn,nkd->qkgd",
        weights_raw.astype(jnp.bfloat16),
        value_three,
        preferred_element_type=jnp.float32,
    )
    mixed = mixed / jnp.transpose(totals, (2, 0, 1))[..., None]
    lang_attended = mixed.reshape(slot_count, -1).astype(jnp.bfloat16)
    out_terms = jnp.dot(lang_attended, l_out, preferred_element_type=jnp.float32)
    summed_out = lax.psum_scatter(
        out_terms.astype(jnp.bfloat16), "tp", scatter_dimension=1, tiled=True
    ).astype(jnp.float32)
    return (filled.astype(jnp.float32) + summed_out).astype(jnp.bfloat16)


def solution(mesh):
    in_specs = (
        P("seq", None),
        P(),
        P(),
        P(None, "tp"),
        P(None, "tp"),
        P(None, "tp"),
        P("tp", None),
        P(),
        P("seq", "tp"),
        P("tp", "seq"),
        P(),
        P("seq", "tp"),
        P("seq"),
        P(),
        P(None, "tp"),
        P(None, "tp"),
        P(None, "tp"),
        P("tp", None),
    )
    out_specs = P("seq", "tp")
    return jax.shard_map(body, mesh=mesh, in_specs=in_specs, out_specs=out_specs, check_vma=False)
```

profile of v0, /device:TPU:0, one launch (start us, length us, event | category | flops | bytes accessed | tf_op | source)
XLA Modules:
  0.0 336.9 jit_solution(2363182958501174080)
XLA Ops:
  8.0 1.6 copy.38
  10.0 1.5 convolution_convert_fusion.6
  12.2 0.8 pad_maximum_fusion.1
  13.0 4.3 %collective-permute-start = (bf16[512,320]{0,1:T(8,128)(2,1)}, bf16[512,320]{0,1:T(8,128)(2,1)}, u32[]{:S(2)}, u32[]{:S(2)}) collective-permute-start(bf16[512,320]{0,1:T(8,128)(2,1)} %pad_maximum_fusion.1), channel_id=1, source_target_pairs={{0,8},{8,16},{16,24},{24,32},{32,40},{40,48},{48,56},{56,64},{64,7... | collective-permute-start | bytes 983048 | tf_op jit(solution)/shard_map/ppermute | solution.py:22
  17.3 1.3 collective-permute-start.1
  18.6 1.3 broadcast_in_dim.94
  19.9 1.8 reshape.228
  21.9 1.4 broadcast_compare_fusion
  23.4 2.2 convolution_convert_fusion.4
  25.6 7.6 %collective-permute-done.1 = bf16[512,320]{0,1:T(8,128)(2,1)} collective-permute-done((bf16[512,320]{0,1:T(8,128)(2,1)}, bf16[512,320]{0,1:T(8,128)(2,1)}, u32[]{:S(2)}, u32[]{:S(2)}) %collective-permute-start.1) | collective-permute-done | bytes 327712 | tf_op jit(solution)/shard_map/ppermute | solution.py:24
  33.3 1.2 pad_maximum_fusion
  34.4 1.0 fusion.134
  35.5 4.7 %fusion.135 = f32[2,512]{1,0:T(2,128)S(1)} fusion(pred[512,1536]{1,0:T(8,128)(4,1)} %broadcast_compare_fusion, bf16[512,2,80]{0,2,1:T(8,128)(2,1)} %bitcast.108, bf16[1536,2,80]{0,2,1:T(8,128)(2,1)} %bitcast.99), kind=kOutput, calls=%fused_computation.174 | convolution fusion | flops 259524096 | bytes 1445888 | tf_op jit(solution)/shard_map/sub | solution.py:76
  40.2 5.5 %fusion.19 = bf16[512,2,80]{0,2,1:T(8,128)(2,1)} fusion(bf16[1536,2,80]{0,2,1:T(8,128)(2,1)} %bitcast.101, f32[512,2]{0,1:T(2,128)S(1)} %bitcast.110, pred[512,1536]{1,0:T(8,128)(4,1)} %broadcast_compare_fusion, bf16[512,2,80]{0,2,1:T(8,128)(2,1)} %bitcast.109, bf16[1536,2,80]{0,2,1:T(8,128)(2,1)} %bitcast.100), kind=kOutput, calls=%fused_computation.32 | convolution fusion | flops 511347200 | bytes 2101248 | tf_op jit(solution)/shard_map/hqn,nhd->qhd/dot_general | solution.py:78
  45.7 2.7 convolution_convert_fusion.2
  48.4 2.4 copy.39
  50.8 6.3 %all-to-all-start = ((bf16[8,512,160]{1,2,0:T(8,128)(2,1)}), bf16[8,512,160]{1,2,0:T(8,128)(2,1)}, u32[]{:S(2)}, u32[]{:S(2)}) async-start(bf16[8,512,160]{1,2,0:T(8,128)(2,1)} %bitcast.95), calls=%async_computation | async-start | bytes 2621440 | tf_op jit(solution)/shard_map/all_to_all | solution.py:39
  57.1 1.9 convert_element_type.82
  59.0 17.0 %all-to-all-done = bf16[8,512,160]{1,2,0:T(8,128)(2,1)} async-done(((bf16[8,512,160]{1,2,0:T(8,128)(2,1)}), bf16[8,512,160]{1,2,0:T(8,128)(2,1)}, u32[]{:S(2)}, u32[]{:S(2)}) %all-to-all-start) | async-done | bytes 1310752 | tf_op jit(solution)/shard_map/all_to_all | solution.py:39
  76.0 1.5 convert_reduce_fusion
  77.5 1.0 multiply_reduce_fusion.1
  79.2 3.3 all-to-all-start.1
  82.5 0.8 dynamic_slice.27
  83.3 4.5 %all-to-all-done.1 = f32[8,1,512]{2,1,0:T(1,128)S(1)} async-done(((f32[8,1,512]{2,1,0:T(1,128)}), f32[8,1,512]{2,1,0:T(1,128)S(1)}, u32[]{:S(2)}, u32[]{:S(2)}) %all-to-all-start.1) | async-done | bytes 16416 | tf_op jit(solution)/shard_map/all_to_all | solution.py:45
  87.8 1.1 multiply_convert_fusion.1
  89.0 21.2 %all_to_all.26 = bf16[8,512,160]{1,2,0:T(8,128)(2,1)S(1)} all-to-all(bf16[8,512,160]{1,2,0:T(8,128)(2,1)S(1)} %broadcast_in_dim.99), channel_id=1, replica_groups=mesh['seq'=16,'tp'=8] {'tp'}, dimensions={0} | all-to-all | bytes 2621440 | tf_op jit(solution)/shard_map/all_to_all | solution.py:45
  110.2 3.0 copy.41
  113.2 4.4 %reshape_reshape.3 = bf16[128,5120]{1,0:T(8,128)(2,1)S(1)} reshape(bf16[512,8,160]{2,1,0:T(8,128)(2,1)} %copy.41) | data formatting | bytes 2621440 | tf_op jit(solution)/shard_map/reshape;reshape | solution.py:144
  117.7 48.6 %all-gather.6.cloned.1.call-done = bf16[640,8192]{1,0:T(8,128)(2,1)} async-done(((bf16[640,512]{1,0:T(8,128)(2,1)}), bf16[640,8192]{1,0:T(8,128)(2,1)}) %all-gather.6.cloned.1.call-update) | async-done | bytes 10485776 | tf_op jit(solution)/shard_map/all_gather | solution.py:153
  166.3 10.7 %convolution_convert_fusion.1 = bf16[128,8192]{1,0:T(8,128)(2,1)} fusion(bf16[640,8192]{1,0:T(8,128)(2,1)} %all-gather.6.cloned.1.call-done, bf16[128,5120]{1,0:T(8,128)(2,1)S(1)} %reshape_reshape.3, bf16[5120,640]{1,0:T(8,128)(2,1)} %all-gather.4.cloned.1.call-done), kind=kOutput, calls=%fused_computation.6 | convolution fusion | flops 2187411456 | bytes 20447232 | tf_op jit(solution)/shard_map/dot_general | solution.py:151
  177.1 3.2 copy.59
  180.3 4.6 %all-to-all-start.3 = ((bf16[8,128,1024]{2,1,0:T(8,128)(2,1)}), bf16[8,128,1024]{2,1,0:T(8,128)(2,1)}, u32[]{:S(2)}, u32[]{:S(2)}) async-start(bf16[8,128,1024]{2,1,0:T(8,128)(2,1)} %bitcast.94), calls=%async_computation.3 | async-start | bytes 4194304 | tf_op jit(solution)/shard_map/all_to_all | solution.py:39
  186.7 25.4 %all-to-all-done.3 = bf16[8,128,1024]{2,1,0:T(8,128)(2,1)} async-done(((bf16[8,128,1024]{2,1,0:T(8,128)(2,1)}), bf16[8,128,1024]{2,1,0:T(8,128)(2,1)}, u32[]{:S(2)}, u32[]{:S(2)}) %all-to-all-start.3) | async-done | bytes 2097184 | tf_op jit(solution)/shard_map/all_to_all | solution.py:39
  212.1 2.0 reduce_sum.115
  214.1 2.0 scatter_custom_fusion
  216.0 4.9 %all-to-all-start.4 = ((bf16[16,16,1024]{2,1,0:T(8,128)(2,1)}), bf16[16,16,1024]{2,1,0:T(8,128)(2,1)S(1)}, u32[]{:S(2)}, u32[]{:S(2)}) async-start(bf16[16,16,1024]{2,1,0:T(8,128)(2,1)} %bitcast.15), calls=%async_computation.4 | async-start | bytes 1048576 | tf_op jit(solution)/shard_map/all_to_all | solution.py:172
  221.8 10.3 %all-to-all-done.4 = bf16[16,16,1024]{2,1,0:T(8,128)(2,1)S(1)} async-done(((bf16[16,16,1024]{2,1,0:T(8,128)(2,1)}), bf16[16,16,1024]{2,1,0:T(8,128)(2,1)S(1)}, u32[]{:S(2)}, u32[]{:S(2)}) %all-to-all-start.4) | async-done | bytes 524320 | tf_op jit(solution)/shard_map/all_to_all | solution.py:172
  232.2 0.8 copy-done.8
  232.9 2.3 scatter_custom_fusion.1
  235.3 0.9 slice_select_fusion
  236.6 28.0 %all-gather.8.cloned.1.call-done = bf16[256,8192]{1,0:T(8,128)(2,1)} async-done(((bf16[256,1024]{1,0:T(8,128)(2,1)}), bf16[256,8192]{1,0:T(8,128)(2,1)}) %all-gather.8.cloned.1.call-update) | async-done | bytes 4194320 | tf_op jit(solution)/shard_map/all_gather | solution.py:193
  264.6 3.3 fusion.1
  268.1 5.8 %fusion.18 = bf16[32,4,8,128]{3,2,1,0:T(8,128)(2,1)S(1)} fusion(bf16[8192,512]{1,0:T(8,128)(2,1)} %param.32, bf16[256,8192]{1,0:T(8,128)(2,1)S(1)} %copy-done.2, f32[8192]{0:T(1024)S(1)} %copy-done.13, f32[256]{0:T(256)S(1)} %add_rsqrt_fusion.2), kind=kOutput, calls=%fused_computation.31 | convolution fusion | flops 2156003328 | bytes 12878848 | tf_op jit(solution)/shard_map/dot_general | solution.py:195
  273.9 3.8 %fusion.136 = (f32[4,256]{1,0:T(4,128)S(1)}, f32[1,4,256,256]{2,3,1,0:T(8,128)S(1)}) fusion(bf16[32,4,8,128]{3,2,1,0:T(8,128)(2,1)S(1)} %fusion.18, bf16[8192,128]{1,0:T(8,128)(2,1)S(1)} %copy-done, bf16[256,8192]{1,0:T(8,128)(2,1)} %all-gather.8.cloned.1.call-done, f32[8192]{0:T(1024)S(1)} %copy-done.13, f32[256]{0:T(256)S(1)} %add_rsqrt_fusion.2, ...), kind=kOutput, calls=%fused_computation.175 | convolution fusion | flops 613186560 | bytes 7705600 | tf_op jit(solution)/shard_map/qkgd,nkd->kgqn/dot_general | solution.py:211
  277.9 4.5 %fusion.28 = bf16[256,1,4,128]{0,3,2,1:T(8,128)(2,1)S(1)} fusion(bf16[8192,128]{1,0:T(8,128)(2,1)} %param.34, f32[1,4,256,256]{2,3,1,0:T(8,128)S(1)} %get-tuple-element.11, f32[4,256]{1,0:T(4,128)S(1)} %get-tuple-element.10, pred[256,256]{0,1:T(8,128)(4,1)S(1)} %fusion.53, f32[256,4]{0,1:T(4,128)S(1)} %bitcast.106, ...), kind=kOutput, calls=%fused_computation.46 | convolution fusion | flops 613449728 | bytes 7709696 | tf_op jit(solution)/shard_map/kgqn,nkd->qkgd/dot_general | solution.py:218
  282.5 7.7 %convolution_convert_fusion = bf16[256,8192]{1,0:T(8,128)(2,1)} fusion(bf16[256,512]{0,1:T(8,128)(2,1)S(1)} %bitcast.102, bf16[512,8192]{1,0:T(8,128)(2,1)} %param.35), kind=kOutput, calls=%fused_computation.5 | convolution fusion | flops 2149580800 | bytes 12845056 | tf_op jit(solution)/shard_map/dot_general | solution.py:226
  290.2 38.1 %reduce-scatter.2.cloned.1.call-done = bf16[256,1024]{1,0:T(8,128)(2,1)} async-done(((bf16[256,8192]{1,0:T(8,128)(2,1)}), bf16[256,1024]{1,0:T(8,128)(2,1)}) %reduce-scatter.2.cloned.1.call-update) | async-done | bytes 524304 | tf_op jit(solution)/shard_map/reduce_scatter | solution.py:227
  328.3 2.0 add_convert_fusion
  (64 shorter events, 7.0 us)
Async XLA Ops:
  6.5 267.3 %copy-start = (bf16[8192,128]{1,0:T(8,128)(2,1)S(1)}, bf16[8192,128]{1,0:T(8,128)(2,1)}, u32[]{:S(2)}) copy-start(bf16[8192,128]{1,0:T(8,128)(2,1)} %param.33) | copy-start | bytes 6291460
  6.5 3.5 %copy-start.14 = (f32[1280]{0:T(1024)S(1)}, f32[1280]{0:T(1024)}, u32[]{:S(2)}) copy-start(f32[1280]{0:T(1024)} %param.20) | copy-start | bytes 15364
  6.5 111.1 %all-gather.4.cloned.1.call-start = ((), (), s32[]{:S(2)}) async-start(), calls=%async_computation.6 | async-start | bytes 6963200 | tf_op jit(solution)/shard_map/all_gather | solution.py:147
  7.3 159.1 %all-gather.6.cloned.1.call-start = ((), (), s32[]{:S(2)}) async-start(), calls=%async_computation.7 | async-start | bytes 11141120 | tf_op jit(solution)/shard_map/all_gather | solution.py:153
  9.6 1.9 copy-start.12
  10.0 8.6 %copy-start.10 = (s32[2048]{0:T(1024)S(1)}, s32[2048]{0:T(1024)}, u32[]{:S(2)}) copy-start(s32[2048]{0:T(1024)} %param.19) | copy-start | bytes 24580
  11.6 0.7 copy-start.3
  12.2 0.8 copy-start.5
  13.0 12.6 %collective-permute-start = (bf16[512,320]{0,1:T(8,128)(2,1)}, bf16[512,320]{0,1:T(8,128)(2,1)}, u32[]{:S(2)}, u32[]{:S(2)}) collective-permute-start(bf16[512,320]{0,1:T(8,128)(2,1)} %pad_maximum_fusion.1), channel_id=1, source_target_pairs={{0,8},{8,16},{16,24},{24,32},{32,40},{40,48},{48,56},{56,64},{64,7... | collective-permute-start | bytes 983048 | tf_op jit(solution)/shard_map/ppermute | solution.py:22
  17.3 16.0 %collective-permute-start.1 = (bf16[512,320]{0,1:T(8,128)(2,1)}, bf16[512,320]{0,1:T(8,128)(2,1)}, u32[]{:S(2)}, u32[]{:S(2)}) collective-permute-start(bf16[512,320]{0,1:T(8,128)(2,1)} %pad_maximum_fusion.1), channel_id=1, source_target_pairs={{8,0},{16,8},{24,16},{32,24},{40,32},{48,40},{56,48},{64,56},{72,6... | collective-permute-start | bytes 983048 | tf_op jit(solution)/shard_map/ppermute | solution.py:24
  21.8 11.5 %copy-start.4 = (bf16[512,160]{0,1:T(8,128)(2,1)S(1)}, bf16[512,160]{0,1:T(8,128)(2,1)}, u32[]{:S(2)}) copy-start(bf16[512,160]{0,1:T(8,128)(2,1)} %copy-done.3) | copy-start | bytes 491524
  21.8 11.5 %copy-start.6 = (bf16[512,160]{0,1:T(8,128)(2,1)S(1)}, bf16[512,160]{0,1:T(8,128)(2,1)}, u32[]{:S(2)}) copy-start(bf16[512,160]{0,1:T(8,128)(2,1)} %copy-done.5) | copy-start | bytes 491524
  50.8 25.1 %all-to-all-start = ((bf16[8,512,160]{1,2,0:T(8,128)(2,1)}), bf16[8,512,160]{1,2,0:T(8,128)(2,1)}, u32[]{:S(2)}, u32[]{:S(2)}) async-start(bf16[8,512,160]{1,2,0:T(8,128)(2,1)} %bitcast.95), calls=%async_computation | async-start | bytes 2621440 | tf_op jit(solution)/shard_map/all_to_all | solution.py:39
  79.2 8.6 %all-to-all-start.1 = ((f32[8,1,512]{2,1,0:T(1,128)}), f32[8,1,512]{2,1,0:T(1,128)S(1)}, u32[]{:S(2)}, u32[]{:S(2)}) async-start(f32[8,1,512]{2,1,0:T(1,128)} %broadcast_in_dim.98), calls=%async_computation.1 | async-start | bytes 32768 | tf_op jit(solution)/shard_map/all_to_all | solution.py:45
  180.3 4.6 %copy-start.9 = (s32[2048,1]{0,1:T(1,128)S(1)}, s32[2048,1]{0,1:T(1,128)}, u32[]{:S(2)}) copy-start(s32[2048,1]{0,1:T(1,128)} %param.28) | copy-start | bytes 24580
  180.3 31.8 %all-to-all-start.3 = ((bf16[8,128,1024]{2,1,0:T(8,128)(2,1)}), bf16[8,128,1024]{2,1,0:T(8,128)(2,1)}, u32[]{:S(2)}, u32[]{:S(2)}) async-start(bf16[8,128,1024]{2,1,0:T(8,128)(2,1)} %bitcast.94), calls=%async_computation.3 | async-start | bytes 4194304 | tf_op jit(solution)/shard_map/all_to_all | solution.py:39
  186.7 48.6 %copy-start.7 = (bf16[256,1024]{1,0:T(8,128)(2,1)S(1)}, bf16[256,1024]{1,0:T(8,128)(2,1)}, u32[]{:S(2)}) copy-start(bf16[256,1024]{1,0:T(8,128)(2,1)} %param.29) | copy-start | bytes 1572868
  186.7 49.8 %copy-start.11 = (s32[256]{0:T(256)S(1)}, s32[256]{0:T(256)}, u32[]{:S(2)}) copy-start(s32[256]{0:T(256)} %param.30) | copy-start | bytes 3076
  216.0 16.1 %all-to-all-start.4 = ((bf16[16,16,1024]{2,1,0:T(8,128)(2,1)}), bf16[16,16,1024]{2,1,0:T(8,128)(2,1)S(1)}, u32[]{:S(2)}, u32[]{:S(2)}) async-start(bf16[16,16,1024]{2,1,0:T(8,128)(2,1)} %bitcast.15), calls=%async_computation.4 | async-start | bytes 1048576 | tf_op jit(solution)/shard_map/all_to_all | solution.py:172
  221.0 43.6 %all-gather.8.cloned.1.call-start = ((), (), s32[]{:S(2)}) async-start(), calls=%async_computation.8 | async-start | bytes 4718592 | tf_op jit(solution)/shard_map/all_gather | solution.py:193
  232.2 0.8 copy-start.8
  235.3 32.6 %copy-start.13 = (f32[8192]{0:T(1024)S(1)}, f32[8192]{0:T(1024)}, u32[]{:S(2)}) copy-start(f32[8192]{0:T(1024)} %param.31) | copy-start | bytes 98308
  236.2 92.1 %reduce-scatter.2.cloned.1.call-start = ((), (), s32[]{:S(2)}) async-start(), calls=%async_computation.9 | async-start | bytes 4718592 | tf_op jit(solution)/shard_map/reduce_scatter | solution.py:227
  264.6 3.4 %copy-start.2 = (bf16[256,8192]{1,0:T(8,128)(2,1)S(1)}, bf16[256,8192]{1,0:T(8,128)(2,1)}, u32[]{:S(2)}) copy-start(bf16[256,8192]{1,0:T(8,128)(2,1)} %all-gather.8.cloned.1.call-done) | copy-start | bytes 12582916
  290.2 38.2 %copy-start.1 = (bf16[256,1024]{1,0:T(8,128)(2,1)S(1)}, bf16[256,1024]{1,0:T(8,128)(2,1)}, u32[]{:S(2)}) copy-start(bf16[256,1024]{1,0:T(8,128)(2,1)} %slice_select_fusion) | copy-start | bytes 1572868
Sparse Core Ops, SparseCore 0:
  9.5 67.2 all-gather.3
  78.9 87.3 all-gather.5
  236.3 28.2 all-gather.7
  290.3 37.9 reduce-scatter.1
where the time goes:
time: 338 us; the launch traced here: 337 us
  waiting for transfers between devices  181 us (54%)
  matrix products  49.8 us (15%)
  local copies, waits for them, and re-layouts  26.1 us (8%)
  starting transfers between devices  25.1 us (7%)
  blocking collectives  21.2 us (6%)
  other arithmetic  20.2 us (6%)
  between operations  13.4 us (4%)
    all_gather x1, waiting for transfers between devices, body(): lax.all_gather(merge_down, 'seq', axis=1, tiled=True)  48.6 us
    all_to_all x2, waiting for transfers between devices, sum_at_owner(): lax.all_to_all(pieces, axis, split_axis=0, concat_axis=0, tiled=True)  42.3 us
    reduce_scatter x1, waiting for transfers between devices, body(): lax.psum_scatter(out_terms.astype(jnp.bfloat16), 'tp', scatter_dimension=...  38.1 us
    all_gather x1, waiting for transfers between devices, body(): full_rows = lax.all_gather(filled, 'tp', axis=1, tiled=True)  28 us
    all_to_all x1, blocking collectives, from_everyone(): return lax.all_to_all(copies, axis, split_axis=0, concat_axis=0, tiled=True)  21.2 us
    all_to_all x2, starting transfers between devices, sum_at_owner(): lax.all_to_all(pieces, axis, split_axis=0, concat_axis=0, tiled=True)  10.8 us
    dot_general x1, matrix products, body(): jnp.dot(hidden, lax.all_gather(merge_down, 'seq', axis=1, tiled=True), pr...  10.7 us
    all_to_all x1, waiting for transfers between devices, body(): lax.all_to_all(outgoing.reshape(owner_count, pair_cap, feature_width), 's...  10.3 us
  transfers between devices with their start and end apart: 10, of which 9 were waited for; matrix products, arithmetic and copies ran while one was open for 14% of the time, Pallas kernels for 0%

commit v1 on v0

--- a/solution.py
+++ b/solution.py
@@ -190,7 +190,9 @@
     )
     is_vision = jnp.arange(slot_count, dtype=jnp.int32) < jnp.sum(from_each)
     filled = jnp.where(is_vision[:, None], vision_slots, text_embed)
-    full_rows = lax.all_gather(filled, "tp", axis=1, tiled=True)
+    full_rows = jnp.concatenate(
+        lax.all_to_all(jnp.stack([filled] * lax.axis_size("tp")), "tp", 0, 0), axis=1
+    )
     lang_normed = rms_scaled(full_rows.astype(jnp.float32), lang_gain)
     lang_query = jnp.dot(lang_normed, l_query, preferred_element_type=jnp.float32).astype(
         jnp.bfloat16

time: 338 us -> 368 us (1.089)
  waiting for transfers between devices: 181 us -> 199 us
  starting transfers between devices: 25.1 us -> 29.7 us
  other arithmetic: 20.2 us -> 24.6 us
    all_to_all x0 -> x1, waiting for transfers between devices: none -> 49.2 us  [body(): lax.all_to_all(jnp.stack([filled] * lax.axis_size('tp')), 'tp', 0, 0)]
    all_gather x1 -> x0, waiting for transfers between devices: 28 us -> none  [body(): full_rows = lax.all_gather(filled, 'tp', axis=1, tiled=True)]
    all_to_all x0 -> x1, starting transfers between devices: none -> 4.68 us  [body(): lax.all_to_all(jnp.stack([filled] * lax.axis_size('tp')), 'tp', 0, 0)]
    reduce_scatter x1, waiting for transfers between devices: 38.1 us -> 34.3 us  [body(): lax.psum_scatter(out_terms.astype(jnp.bfloat16), 'tp', scatter_dimension=...]
  transfers between devices with their start and end apart: 10 -> 10, of which waited for: 9 -> 9; matrix products, arithmetic and copies ran while one was open for 14% -> 13% of each run, Pallas kernels for 0% -> 0%
where the time goes in v1:
time: 368 us; the launch traced here: 367 us
  waiting for transfers between devices  199 us (54%)
  matrix products  50.6 us (14%)
  starting transfers between devices  29.7 us (8%)
  local copies, waits for them, and re-layouts  28.9 us (8%)
  other arithmetic  24.6 us (7%)
  blocking collectives  21.2 us (6%)
  between operations  13.4 us (4%)
    all_to_all x1, waiting for transfers between devices, body(): lax.all_to_all(jnp.stack([filled] * lax.axis_size('tp')), 'tp', 0, 0)  49.2 us
    all_gather x1, waiting for transfers between devices, body(): lax.all_gather(merge_down, 'seq', axis=1, tiled=True)  48.6 us
    all_to_all x2, waiting for transfers between devices, sum_at_owner(): lax.all_to_all(pieces, axis, split_axis=0, concat_axis=0, tiled=True)  42.4 us
    reduce_scatter x1, waiting for transfers between devices, body(): lax.psum_scatter(out_terms.astype(jnp.bfloat16), 'tp', scatter_dimension=...  34.3 us
    all_to_all x1, blocking collectives, from_everyone(): return lax.all_to_all(copies, axis, split_axis=0, concat_axis=0, tiled=True)  21.2 us
    all_to_all x2, starting transfers between devices, sum_at_owner(): lax.all_to_all(pieces, axis, split_axis=0, concat_axis=0, tiled=True)  10.8 us
    dot_general x1, matrix products, body(): jnp.dot(hidden, lax.all_gather(merge_down, 'seq', axis=1, tiled=True), pr...  10.7 us
    all_to_all x1, waiting for transfers between devices, body(): lax.all_to_all(outgoing.reshape(owner_count, pair_cap, feature_width), 's...  10.4 us
  transfers between devices with their start and end apart: 10, of which 9 were waited for; matrix products, arithmetic and copies ran while one was open for 13% of the time, Pallas kernels for 0%

profile of v1, /device:TPU:0, one launch (start us, length us, event | category | flops | bytes accessed | tf_op | source)
XLA Modules:
  0.0 367.1 jit_solution(5451829484039944341)
XLA Ops:
  8.0 1.6 copy.41
  10.0 1.5 convolution_convert_fusion.6
  13.0 4.3 %collective-permute-start = (bf16[512,320]{0,1:T(8,128)(2,1)}, bf16[512,320]{0,1:T(8,128)(2,1)}, u32[]{:S(2)}, u32[]{:S(2)}) collective-permute-start(bf16[512,320]{0,1:T(8,128)(2,1)} %pad_maximum_fusion.1), channel_id=1, source_target_pairs={{0,8},{8,16},{16,24},{24,32},{32,40},{40,48},{48,56},{56,64},{64,7... | collective-permute-start | bytes 983048 | tf_op jit(solution)/shard_map/ppermute | solution.py:22
  17.3 1.3 collective-permute-start.1
  18.6 1.3 broadcast_in_dim.94
  19.9 1.8 reshape.234
  21.9 1.4 broadcast_compare_fusion
  23.4 2.2 convolution_convert_fusion.4
  25.6 7.6 %collective-permute-done.1 = bf16[512,320]{0,1:T(8,128)(2,1)} collective-permute-done((bf16[512,320]{0,1:T(8,128)(2,1)}, bf16[512,320]{0,1:T(8,128)(2,1)}, u32[]{:S(2)}, u32[]{:S(2)}) %collective-permute-start.1) | collective-permute-done | bytes 327712 | tf_op jit(solution)/shard_map/ppermute | solution.py:24
  33.3 1.2 pad_maximum_fusion
  35.5 4.7 %fusion.129 = f32[2,512]{1,0:T(2,128)S(1)} fusion(pred[512,1536]{1,0:T(8,128)(4,1)} %broadcast_compare_fusion, bf16[512,2,80]{0,2,1:T(8,128)(2,1)} %bitcast.119, bf16[1536,2,80]{0,2,1:T(8,128)(2,1)} %bitcast.110), kind=kOutput, calls=%fused_computation.173 | convolution fusion | flops 259524096 | bytes 1445888 | tf_op jit(solution)/shard_map/sub | solution.py:76
  40.2 5.5 %fusion.18 = bf16[512,2,80]{0,2,1:T(8,128)(2,1)} fusion(bf16[1536,2,80]{0,2,1:T(8,128)(2,1)} %bitcast.112, f32[512,2]{0,1:T(2,128)S(1)} %bitcast.121, pred[512,1536]{1,0:T(8,128)(4,1)} %broadcast_compare_fusion, bf16[512,2,80]{0,2,1:T(8,128)(2,1)} %bitcast.120, bf16[1536,2,80]{0,2,1:T(8,128)(2,1)} %bitcast.111), kind=kOutput, calls=%fused_computation.31 | convolution fusion | flops 511347200 | bytes 2101248 | tf_op jit(solution)/shard_map/hqn,nhd->qhd/dot_general | solution.py:78
  45.7 2.7 convolution_convert_fusion.2
  48.4 2.4 copy.42
  50.8 6.3 %all-to-all-start = ((bf16[8,512,160]{1,2,0:T(8,128)(2,1)}), bf16[8,512,160]{1,2,0:T(8,128)(2,1)}, u32[]{:S(2)}, u32[]{:S(2)}) async-start(bf16[8,512,160]{1,2,0:T(8,128)(2,1)} %bitcast.106), calls=%async_computation | async-start | bytes 2621440 | tf_op jit(solution)/shard_map/all_to_all | solution.py:39
  57.1 1.9 convert_element_type.92
  59.0 17.0 %all-to-all-done = bf16[8,512,160]{1,2,0:T(8,128)(2,1)} async-done(((bf16[8,512,160]{1,2,0:T(8,128)(2,1)}), bf16[8,512,160]{1,2,0:T(8,128)(2,1)}, u32[]{:S(2)}, u32[]{:S(2)}) %all-to-all-start) | async-done | bytes 1310752 | tf_op jit(solution)/shard_map/all_to_all | solution.py:39
  76.0 1.5 convert_reduce_fusion
  79.2 3.3 all-to-all-start.1
  83.3 4.5 %all-to-all-done.1 = f32[8,1,512]{2,1,0:T(1,128)S(1)} async-done(((f32[8,1,512]{2,1,0:T(1,128)}), f32[8,1,512]{2,1,0:T(1,128)S(1)}, u32[]{:S(2)}, u32[]{:S(2)}) %all-to-all-start.1) | async-done | bytes 16416 | tf_op jit(solution)/shard_map/all_to_all | solution.py:45
  87.8 1.1 multiply_convert_fusion.1
  89.0 21.2 %all_to_all.31 = bf16[8,512,160]{1,2,0:T(8,128)(2,1)S(1)} all-to-all(bf16[8,512,160]{1,2,0:T(8,128)(2,1)S(1)} %broadcast_in_dim.99), channel_id=1, replica_groups=mesh['seq'=16,'tp'=8] {'tp'}, dimensions={0} | all-to-all | bytes 2621440 | tf_op jit(solution)/shard_map/all_to_all | solution.py:45
  110.2 3.0 copy.44
  113.2 4.4 %reshape_reshape.3 = bf16[128,5120]{1,0:T(8,128)(2,1)S(1)} reshape(bf16[512,8,160]{2,1,0:T(8,128)(2,1)} %copy.44) | data formatting | bytes 2621440 | tf_op jit(solution)/shard_map/reshape;reshape | solution.py:144
  117.7 48.6 %all-gather.5.cloned.1.call-done = bf16[640,8192]{1,0:T(8,128)(2,1)} async-done(((bf16[640,512]{1,0:T(8,128)(2,1)}), bf16[640,8192]{1,0:T(8,128)(2,1)}) %all-gather.5.cloned.1.call-update) | async-done | bytes 10485776 | tf_op jit(solution)/shard_map/all_gather | solution.py:153
  166.3 10.7 %convolution_convert_fusion.1 = bf16[128,8192]{1,0:T(8,128)(2,1)} fusion(bf16[640,8192]{1,0:T(8,128)(2,1)} %all-gather.5.cloned.1.call-done, bf16[128,5120]{1,0:T(8,128)(2,1)S(1)} %reshape_reshape.3, bf16[5120,640]{1,0:T(8,128)(2,1)} %all-gather.3.cloned.1.call-done), kind=kOutput, calls=%fused_computation.4 | convolution fusion | flops 2187411456 | bytes 20447232 | tf_op jit(solution)/shard_map/dot_general | solution.py:151
  177.1 3.2 copy.63
  180.3 4.6 %all-to-all-start.3 = ((bf16[8,128,1024]{2,1,0:T(8,128)(2,1)}), bf16[8,128,1024]{2,1,0:T(8,128)(2,1)}, u32[]{:S(2)}, u32[]{:S(2)}) async-start(bf16[8,128,1024]{2,1,0:T(8,128)(2,1)} %bitcast.105), calls=%async_computation.3 | async-start | bytes 4194304 | tf_op jit(solution)/shard_map/all_to_all | solution.py:39
  186.7 25.4 %all-to-all-done.3 = bf16[8,128,1024]{2,1,0:T(8,128)(2,1)} async-done(((bf16[8,128,1024]{2,1,0:T(8,128)(2,1)}), bf16[8,128,1024]{2,1,0:T(8,128)(2,1)}, u32[]{:S(2)}, u32[]{:S(2)}) %all-to-all-start.3) | async-done | bytes 2097184 | tf_op jit(solution)/shard_map/all_to_all | solution.py:39
  212.1 2.0 reduce_sum.115
  214.1 2.0 scatter_custom_fusion
  216.0 4.9 %all-to-all-start.4 = ((bf16[16,16,1024]{2,1,0:T(8,128)(2,1)}), bf16[16,16,1024]{2,1,0:T(8,128)(2,1)S(1)}, u32[]{:S(2)}, u32[]{:S(2)}) async-start(bf16[16,16,1024]{2,1,0:T(8,128)(2,1)} %bitcast.15), calls=%async_computation.4 | async-start | bytes 1048576 | tf_op jit(solution)/shard_map/all_to_all | solution.py:172
  221.8 10.4 %all-to-all-done.4 = bf16[16,16,1024]{2,1,0:T(8,128)(2,1)S(1)} async-done(((bf16[16,16,1024]{2,1,0:T(8,128)(2,1)}), bf16[16,16,1024]{2,1,0:T(8,128)(2,1)S(1)}, u32[]{:S(2)}, u32[]{:S(2)}) %all-to-all-start.4) | async-done | bytes 524320 | tf_op jit(solution)/shard_map/all_to_all | solution.py:172
  232.2 1.8 scatter_custom_fusion.1
  234.0 1.2 slice_select_fusion
  235.3 2.2 stack.2
  237.6 4.7 %all-to-all-start.5 = ((bf16[8,256,1024]{1,2,0:T(8,128)(2,1)}), bf16[8,256,1024]{1,2,0:T(8,128)(2,1)}, u32[]{:S(2)}, u32[]{:S(2)}) async-start(bf16[8,256,1024]{1,2,0:T(8,128)(2,1)} %stack.2), calls=%async_computation.5 | async-start | bytes 8388608 | tf_op jit(solution)/shard_map/all_to_all | solution.py:194
  242.7 49.2 %all-to-all-done.5 = bf16[8,256,1024]{1,2,0:T(8,128)(2,1)} async-done(((bf16[8,256,1024]{1,2,0:T(8,128)(2,1)}), bf16[8,256,1024]{1,2,0:T(8,128)(2,1)}, u32[]{:S(2)}, u32[]{:S(2)}) %all-to-all-start.5) | async-done | bytes 4194336 | tf_op jit(solution)/shard_map/all_to_all | solution.py:194
  291.9 3.3 multiply_reduce_fusion
  295.2 2.9 fusion.2
  298.1 1.9 copy-done.1
  300.0 5.7 %fusion.17 = bf16[32,4,8,128]{3,2,1,0:T(8,128)(2,1)S(1)} fusion(bf16[256,8192]{0,1:T(8,128)(2,1)S(1)} %fusion.2, bf16[8192,512]{1,0:T(8,128)(2,1)} %param.32), kind=kOutput, calls=%fused_computation.30 | convolution fusion | flops 2147614720 | bytes 12845056 | tf_op jit(solution)/shard_map/dot_general | solution.py:197
  305.7 4.7 %fusion.130 = (f32[4,256]{1,0:T(4,128)S(1)}, f32[1,4,256,256]{2,3,1,0:T(8,128)}) fusion(bf16[32,4,8,128]{3,2,1,0:T(8,128)(2,1)S(1)} %fusion.17, bf16[256,8192]{0,1:T(8,128)(2,1)} %copy-done.1, bf16[8192,128]{1,0:T(8,128)(2,1)S(1)} %copy-done, pred[256,256]{0,1:T(8,128)(4,1)S(1)} %fusion.52), kind=kOutput, calls=%fused_computation.174 | convolution fusion | flops 604797952 | bytes 7671808 | tf_op jit(solution)/shard_map/qkgd,nkd->kgqn/dot_general | solution.py:213
  310.4 1.4 fusion.28
  311.9 4.6 %fusion.27 = bf16[256,1,4,128]{0,3,2,1:T(8,128)(2,1)S(1)} fusion(bf16[256,8192]{0,1:T(8,128)(2,1)} %copy-done.1, bf16[8192,128]{1,0:T(8,128)(2,1)} %param.34, f32[1,4,256,256]{2,3,1,0:T(8,128)} %get-tuple-element.11, f32[4,256]{1,0:T(4,128)S(1)} %get-tuple-element.10, pred[256,256]{0,1:T(8,128)(4,1)S(1)} %fusion.52, f32[256,4]{0,1:T(4,128)S(1)} %bitcast.117), kind=kOutput, calls=%fused_computation.45 | convolution fusion | flops 605061120 | bytes 7675904 | tf_op jit(solution)/shard_map/kgqn,nkd->qkgd/dot_general | solution.py:220
  316.5 7.7 %convolution_convert_fusion = bf16[256,8192]{1,0:T(8,128)(2,1)} fusion(bf16[256,512]{0,1:T(8,128)(2,1)S(1)} %bitcast.113, bf16[512,8192]{1,0:T(8,128)(2,1)} %param.35), kind=kOutput, calls=%fused_computation.3 | convolution fusion | flops 2149580800 | bytes 12845056 | tf_op jit(solution)/shard_map/dot_general | solution.py:228
  324.2 34.3 %reduce-scatter.2.cloned.1.call-done = bf16[256,1024]{1,0:T(8,128)(2,1)} async-done(((bf16[256,8192]{1,0:T(8,128)(2,1)}), bf16[256,1024]{1,0:T(8,128)(2,1)}) %reduce-scatter.2.cloned.1.call-update) | async-done | bytes 524304 | tf_op jit(solution)/shard_map/reduce_scatter | solution.py:229
  358.5 2.0 add_convert_fusion
  (60 shorter events, 10.4 us)
Async XLA Ops:
  6.5 299.2 %copy-start = (bf16[8192,128]{1,0:T(8,128)(2,1)S(1)}, bf16[8192,128]{1,0:T(8,128)(2,1)}, u32[]{:S(2)}) copy-start(bf16[8192,128]{1,0:T(8,128)(2,1)} %param.33) | copy-start | bytes 6291460
  6.5 3.5 copy-start.11
  6.5 111.1 %all-gather.3.cloned.1.call-start = ((), (), s32[]{:S(2)}) async-start(), calls=%async_computation.7 | async-start | bytes 6963200 | tf_op jit(solution)/shard_map/all_gather | solution.py:147
  7.3 159.1 %all-gather.5.cloned.1.call-start = ((), (), s32[]{:S(2)}) async-start(), calls=%async_computation.8 | async-start | bytes 11141120 | tf_op jit(solution)/shard_map/all_gather | solution.py:153
  9.6 1.9 copy-start.10
  10.0 8.6 %copy-start.8 = (s32[2048]{0:T(1024)S(1)}, s32[2048]{0:T(1024)}, u32[]{:S(2)}) copy-start(s32[2048]{0:T(1024)} %param.19) | copy-start | bytes 24580
  11.6 0.7 copy-start.2
  12.2 0.8 copy-start.4
  13.0 12.6 %collective-permute-start = (bf16[512,320]{0,1:T(8,128)(2,1)}, bf16[512,320]{0,1:T(8,128)(2,1)}, u32[]{:S(2)}, u32[]{:S(2)}) collective-permute-start(bf16[512,320]{0,1:T(8,128)(2,1)} %pad_maximum_fusion.1), channel_id=1, source_target_pairs={{0,8},{8,16},{16,24},{24,32},{32,40},{40,48},{48,56},{56,64},{64,7... | collective-permute-start | bytes 983048 | tf_op jit(solution)/shard_map/ppermute | solution.py:22
  17.3 16.0 %collective-permute-start.1 = (bf16[512,320]{0,1:T(8,128)(2,1)}, bf16[512,320]{0,1:T(8,128)(2,1)}, u32[]{:S(2)}, u32[]{:S(2)}) collective-permute-start(bf16[512,320]{0,1:T(8,128)(2,1)} %pad_maximum_fusion.1), channel_id=1, source_target_pairs={{8,0},{16,8},{24,16},{32,24},{40,32},{48,40},{56,48},{64,56},{72,6... | collective-permute-start | bytes 983048 | tf_op jit(solution)/shard_map/ppermute | solution.py:24
  21.8 11.5 %copy-start.3 = (bf16[512,160]{0,1:T(8,128)(2,1)S(1)}, bf16[512,160]{0,1:T(8,128)(2,1)}, u32[]{:S(2)}) copy-start(bf16[512,160]{0,1:T(8,128)(2,1)} %copy-done.2) | copy-start | bytes 491524
  21.8 11.5 %copy-start.5 = (bf16[512,160]{0,1:T(8,128)(2,1)S(1)}, bf16[512,160]{0,1:T(8,128)(2,1)}, u32[]{:S(2)}) copy-start(bf16[512,160]{0,1:T(8,128)(2,1)} %copy-done.4) | copy-start | bytes 491524
  50.8 25.1 %all-to-all-start = ((bf16[8,512,160]{1,2,0:T(8,128)(2,1)}), bf16[8,512,160]{1,2,0:T(8,128)(2,1)}, u32[]{:S(2)}, u32[]{:S(2)}) async-start(bf16[8,512,160]{1,2,0:T(8,128)(2,1)} %bitcast.106), calls=%async_computation | async-start | bytes 2621440 | tf_op jit(solution)/shard_map/all_to_all | solution.py:39
  79.2 8.6 %all-to-all-start.1 = ((f32[8,1,512]{2,1,0:T(1,128)}), f32[8,1,512]{2,1,0:T(1,128)S(1)}, u32[]{:S(2)}, u32[]{:S(2)}) async-start(f32[8,1,512]{2,1,0:T(1,128)} %broadcast_in_dim.98), calls=%async_computation.1 | async-start | bytes 32768 | tf_op jit(solution)/shard_map/all_to_all | solution.py:45
  180.3 4.6 %copy-start.6 = (s32[2048,1]{0,1:T(1,128)S(1)}, s32[2048,1]{0,1:T(1,128)}, u32[]{:S(2)}) copy-start(s32[2048,1]{0,1:T(1,128)} %param.28) | copy-start | bytes 24580
  180.3 31.8 %all-to-all-start.3 = ((bf16[8,128,1024]{2,1,0:T(8,128)(2,1)}), bf16[8,128,1024]{2,1,0:T(8,128)(2,1)}, u32[]{:S(2)}, u32[]{:S(2)}) async-start(bf16[8,128,1024]{2,1,0:T(8,128)(2,1)} %bitcast.105), calls=%async_computation.3 | async-start | bytes 4194304 | tf_op jit(solution)/shard_map/all_to_all | solution.py:39
  216.0 16.1 %all-to-all-start.4 = ((bf16[16,16,1024]{2,1,0:T(8,128)(2,1)}), bf16[16,16,1024]{2,1,0:T(8,128)(2,1)S(1)}, u32[]{:S(2)}, u32[]{:S(2)}) async-start(bf16[16,16,1024]{2,1,0:T(8,128)(2,1)} %bitcast.15), calls=%async_computation.4 | async-start | bytes 1048576 | tf_op jit(solution)/shard_map/all_to_all | solution.py:172
  237.6 5.0 %copy-start.9 = (s32[256]{0:T(256)S(1)}, s32[256]{0:T(256)}, u32[]{:S(2)}) copy-start(s32[256]{0:T(256)} %param.30) | copy-start | bytes 3076
  237.6 54.3 %all-to-all-start.5 = ((bf16[8,256,1024]{1,2,0:T(8,128)(2,1)}), bf16[8,256,1024]{1,2,0:T(8,128)(2,1)}, u32[]{:S(2)}, u32[]{:S(2)}) async-start(bf16[8,256,1024]{1,2,0:T(8,128)(2,1)} %stack.2), calls=%async_computation.5 | async-start | bytes 8388608 | tf_op jit(solution)/shard_map/all_to_all | solution.py:194
  242.3 53.0 %copy-start.7 = (f32[8192]{0:T(1024)S(1)}, f32[8192]{0:T(1024)}, u32[]{:S(2)}) copy-start(f32[8192]{0:T(1024)} %param.31) | copy-start | bytes 98308
  242.3 116.2 %reduce-scatter.2.cloned.1.call-start = ((), (), s32[]{:S(2)}) async-start(), calls=%async_computation.9 | async-start | bytes 4718592 | tf_op jit(solution)/shard_map/reduce_scatter | solution.py:229
  298.1 1.9 copy-start.1
Sparse Core Ops, SparseCore 0:
  9.5 67.2 all-gather.2
  78.9 87.3 all-gather.4
  324.3 34.1 reduce-scatter.1
